TPU v7x, 128 devices: a whole 4x4x4 slice. The times are simulated.
128 devices in a mesh: row: 8 (over y_hi, z), col: 16 (over x, y_lo, core).
Axes of the slice: x: 4, y: 4 (y_hi: 2, y_lo: 2; y = y_hi * 2 + y_lo), z: 4, core: 2. Of those that a mesh axis runs over, the one named last changes fastest.
Arguments:
- grad: float32 [8192, 14336], P(('row', 'col')), may hold values from -30 to 30
- momentum: float32 [8192, 14336], P(('row', 'col')), may hold values from -6 to 6
- weight: float32 [8192, 14336], P(('row', 'col')), may hold values from -0.75 to 0.75
Outputs:
- new_weight: float32 [8192, 14336], P('row', 'col')
- new_momentum: float32 [8192, 14336], P('row', 'col')
All inputs are finite; a program needn't handle non-finite values.
Results may differ from a plain program's by a relative error of at most 0.00002.
Values sent between devices are 32-bit elements; how exact they have to be, the bound alone decides.
A program may use at most 128 MiB of HBM per device.

v0:
```python
import functools
import math

import jax
import jax.numpy as jnp
from jax import lax
from jax.sharding import Mesh
from jax.sharding import PartitionSpec as P

D = 8192
FF = 14336
ROW_COL = ("row_0", "row_1", "col_0", "col_1", "col_2")
COL = ("col_0", "col_1", "col_2")
ROW = ("row_0", "row_1")


def one_axis_at_a_time(shard, axes):
    return functools.reduce(lax.psum, axes, shard)


def split_up(shard, dim, count):
    before, after = (shard.shape[:dim], shard.shape[dim + 1 :])
    return jnp.moveaxis(shard.reshape(*before, count, -1, *after), dim, 0)


def piece_ends(length, count):
    unit = 8 if length >= 8 * count else 1
    return [length // unit * k // count * unit for k in range(1, count)]


def joined_along(blocks, dim):
    lengths = list(blocks.shape[1:])
    lengths[dim] *= blocks.shape[0]
    return jnp.moveaxis(blocks, 0, dim).reshape(lengths)


def exchange_in_pieces(shard, axis, pieces, split_dim, concat_dim):
    blocks = split_up(shard, split_dim, lax.axis_size(axis))
    split_at = max(range(1, max(2, blocks.ndim - 1)), key=lambda d: blocks.shape[d])
    gathered = []
    for section in jnp.split(blocks, piece_ends(blocks.shape[split_at], pieces), axis=split_at):
        if section.size:
            gathered.append(lax.all_to_all(section, axis, split_axis=0, concat_axis=0, tiled=True))
    return joined_along(jnp.concatenate(gathered, axis=split_at), concat_dim)


def update_state(total, grad, momentum, weight):
    limit = jnp.float32(math.sqrt(D * FF))
    factor = jnp.minimum(jnp.float32(1.0), limit / (jnp.sqrt(total) + jnp.float32(1e-06)))
    new_momentum = jnp.float32(0.9) * momentum + factor * grad
    new_weight = weight - jnp.float32(0.1) * new_momentum
    return (new_weight, new_momentum)


def body(grad, momentum, weight):
    total = one_axis_at_a_time(jnp.sum(grad * grad), ROW_COL)
    local_weight, local_momentum = update_state(total, grad, momentum, weight)
    new_weight, new_momentum = (
        exchange_in_pieces(local_weight, COL, 2, 1, 0),
        exchange_in_pieces(local_momentum, COL, 2, 1, 0),
    )
    return (new_weight, new_momentum)


def solution(mesh):
    split = Mesh(mesh.devices.reshape(2, 4, 4, 2, 2), ("row_0", "row_1", "col_0", "col_1", "col_2"))
    return jax.shard_map(
        body,
        mesh=split,
        in_specs=(P(ROW_COL, None), P(ROW_COL, None), P(ROW_COL, None)),
        out_specs=(P(ROW, COL), P(ROW, COL)),
        check_vma=False,
    )
```

profile of v0, /device:TPU:1, one launch (start us, length us, event | category | flops | bytes accessed | tf_op | source)
XLA Modules:
  0.0 172.7 jit_solution(11706589266884815369)
XLA Ops:
  0.6 3.6 %multiply_reduce_fusion = f32[]{:T(128)} fusion(f32[64,14336]{1,0:T(8,128)} %param.3), kind=kLoop, calls=%fused_computation.6 | loop fusion | flops 1835007 | bytes 3670020 | tf_op jit(solution)/shard_map/reduce_sum | solution.py:56
  4.2 6.7 %psum.35 = f32[]{:T(128)} all-reduce(f32[]{:T(128)} %multiply_reduce_fusion), channel_id=1, replica_groups=mesh['row_0'=2,'row_1'=4,'col_0'=4,'col_1'=2,'col_2'=2] {'row_0'}, use_global_device_ids=true, to_apply=%region_1.0 | all-reduce | flops 1 | bytes 8 | tf_op jit(solution)/shard_map/psum | solution.py:18
  10.9 10.4 %psum.36 = f32[]{:T(128)} all-reduce(f32[]{:T(128)} %psum.35), channel_id=1, replica_groups=mesh['row_0'=2,'row_1'=4,'col_0'=4,'col_1'=2,'col_2'=2] {'row_1'}, use_global_device_ids=true, to_apply=%region_2.0 | all-reduce | flops 1 | bytes 8 | tf_op jit(solution)/shard_map/psum | solution.py:18
  21.3 9.1 %psum.37 = f32[]{:T(128)} all-reduce(f32[]{:T(128)} %psum.36), channel_id=1, replica_groups=mesh['row_0'=2,'row_1'=4,'col_0'=4,'col_1'=2,'col_2'=2] {'col_0'}, use_global_device_ids=true, to_apply=%region_3.0 | all-reduce | flops 1 | bytes 8 | tf_op jit(solution)/shard_map/psum | solution.py:18
  30.4 4.4 %psum.38 = f32[]{:T(128)} all-reduce(f32[]{:T(128)} %psum.37), channel_id=1, replica_groups=mesh['row_0'=2,'row_1'=4,'col_0'=4,'col_1'=2,'col_2'=2] {'col_1'}, use_global_device_ids=true, to_apply=%region_4.0 | all-reduce | flops 1 | bytes 8 | tf_op jit(solution)/shard_map/psum | solution.py:18
  34.7 9.8 %psum.39 = f32[]{:T(128)} all-reduce(f32[]{:T(128)} %psum.38), channel_id=1, replica_groups=mesh['row_0'=2,'row_1'=4,'col_0'=4,'col_1'=2,'col_2'=2] {'col_2'}, use_global_device_ids=true, to_apply=%region_5.0 | all-reduce | flops 1 | bytes 8 | tf_op jit(solution)/shard_map/psum | solution.py:18
  45.2 6.8 %multiply_subtract_fusion = (f32[64,14336]{1,0:T(8,128)S(1)}, f32[64,14336]{1,0:T(8,128)}) fusion(f32[64,14336]{1,0:T(8,128)} %param.5, f32[64,14336]{1,0:T(8,128)} %param.3, f32[]{:T(128)S(6)} %min_shard_map.3, f32[64,14336]{1,0:T(8,128)} %param.4), kind=kLoop, calls=%fused_computation.4 | loop fusion | flops 4587520 | bytes 18350084 | tf_op jit(solution)/shard_map/sub | solution.py:51
  52.0 0.4 copy.12
  52.4 1.5 fusion.1
  53.9 27.5 %all_to_all.20 = f32[16,32,896]{2,1,0:T(8,128)S(1)} all-to-all(f32[16,32,896]{2,1,0:T(8,128)S(1)} %get-tuple-element.6), channel_id=1, replica_groups=mesh['row_0'=2,'row_1'=4,'col_0'=4,'col_1'=2,'col_2'=2] {'col_0','col_1'..., dimensions={0} | all-to-all | bytes 3670016 | tf_op jit(solution)/shard_map/all_to_all | solution.py:43
  81.4 4.5 %all-to-all-start.1 = ((f32[16,32,896]{2,1,0:T(8,128)}), f32[16,32,896]{2,1,0:T(8,128)}, u32[]{:S(2)}, u32[]{:S(2)}) async-start(f32[16,32,896]{2,1,0:T(8,128)} %get-tuple-element.7), calls=%async_computation.1 | async-start | bytes 3670016 | tf_op jit(solution)/shard_map/all_to_all | solution.py:43
  86.0 2.4 %copy.11 = f32[8,16,8,896]{3,2,0,1:T(8,128)S(1)} copy(f32[8,16,8,896]{3,2,1,0:T(8,128)} %bitcast.18) | data formatting | bytes 7340032 | tf_op jit(solution)/shard_map/reshape | solution.py:23
  88.4 2.1 %fusion = (f32[16,32,896]{2,1,0:T(8,128)}, f32[16,32,896]{2,1,0:T(8,128)}) fusion(f32[16,64,896]{2,1,0:T(8,128)S(1)} %bitcast.17), kind=kLoop, calls=%fused_computation.7 | loop fusion | bytes 7340032 | tf_op jit(solution)/shard_map/split | solution.py:41
  90.5 19.6 %all-to-all-done.1 = f32[16,32,896]{2,1,0:T(8,128)} async-done(((f32[16,32,896]{2,1,0:T(8,128)}), f32[16,32,896]{2,1,0:T(8,128)}, u32[]{:S(2)}, u32[]{:S(2)}) %all-to-all-start.1) | async-done | bytes 1835040 | tf_op jit(solution)/shard_map/all_to_all | solution.py:43
  110.2 29.5 %all_to_all.21 = f32[16,32,896]{2,1,0:T(8,128)} all-to-all(f32[16,32,896]{2,1,0:T(8,128)} %get-tuple-element.4), channel_id=1, replica_groups=mesh['row_0'=2,'row_1'=4,'col_0'=4,'col_1'=2,'col_2'=2] {'col_0','col_1'..., dimensions={0} | all-to-all | bytes 3670016 | tf_op jit(solution)/shard_map/all_to_all | solution.py:43
  139.7 4.6 %all-to-all-start.3 = ((f32[16,32,896]{2,1,0:T(8,128)}), f32[16,32,896]{2,1,0:T(8,128)}, u32[]{:S(2)}, u32[]{:S(2)}) async-start(f32[16,32,896]{2,1,0:T(8,128)} %get-tuple-element.5), calls=%async_computation.3 | async-start | bytes 3670016 | tf_op jit(solution)/shard_map/all_to_all | solution.py:43
  144.3 3.7 %pad_maximum_fusion = f32[16,64,896]{2,1,0:T(8,128)} fusion(f32[16,32,896]{2,1,0:T(8,128)} %all-to-all-done.1, f32[16,32,896]{2,1,0:T(8,128)S(1)} %all_to_all.20), kind=kLoop, calls=%fused_computation.2 | loop fusion | flops 917504 | bytes 7340032 | tf_op jit(solution)/shard_map/concatenate | solution.py:44
  147.9 20.5 %all-to-all-done.3 = f32[16,32,896]{2,1,0:T(8,128)} async-done(((f32[16,32,896]{2,1,0:T(8,128)}), f32[16,32,896]{2,1,0:T(8,128)}, u32[]{:S(2)}, u32[]{:S(2)}) %all-to-all-start.3) | async-done | bytes 1835040 | tf_op jit(solution)/shard_map/all_to_all | solution.py:43
  168.5 4.2 %pad_maximum_fusion.1 = f32[16,64,896]{2,1,0:T(8,128)} fusion(f32[16,32,896]{2,1,0:T(8,128)} %all-to-all-done.3, f32[16,32,896]{2,1,0:T(8,128)} %all_to_all.21), kind=kLoop, calls=%fused_computation.3 | loop fusion | flops 917504 | bytes 7340032 | tf_op jit(solution)/shard_map/concatenate | solution.py:44
Async XLA Ops:
  81.4 28.7 %all-to-all-start.1 = ((f32[16,32,896]{2,1,0:T(8,128)}), f32[16,32,896]{2,1,0:T(8,128)}, u32[]{:S(2)}, u32[]{:S(2)}) async-start(f32[16,32,896]{2,1,0:T(8,128)} %get-tuple-element.7), calls=%async_computation.1 | async-start | bytes 3670016 | tf_op jit(solution)/shard_map/all_to_all | solution.py:43
  139.7 28.8 %all-to-all-start.3 = ((f32[16,32,896]{2,1,0:T(8,128)}), f32[16,32,896]{2,1,0:T(8,128)}, u32[]{:S(2)}, u32[]{:S(2)}) async-start(f32[16,32,896]{2,1,0:T(8,128)} %get-tuple-element.5), calls=%async_computation.3 | async-start | bytes 3670016 | tf_op jit(solution)/shard_map/all_to_all | solution.py:43
where the time goes:
time: 173 us
  blocking collectives  97.3 us (56%)
  waiting for transfers between devices  40.2 us (23%)
  other arithmetic  18.3 us (11%)
  starting transfers between devices  9.11 us (5%)
  local copies, waits for them, and re-layouts  6.42 us (4%)
    all_to_all x2, blocking collectives, exchange_in_pieces(): lax.all_to_all(section, axis, split_axis=0, concat_axis=0, tiled=True)  57 us
    psum x5, blocking collectives, one_axis_at_a_time(): return functools.reduce(lax.psum, axes, shard)  40.3 us
    all_to_all x2, waiting for transfers between devices, exchange_in_pieces(): lax.all_to_all(section, axis, split_axis=0, concat_axis=0, tiled=True)  40.2 us
    all_to_all x2, starting transfers between devices, exchange_in_pieces(): lax.all_to_all(section, axis, split_axis=0, concat_axis=0, tiled=True)  9.11 us
    concatenate x2, other arithmetic, exchange_in_pieces(): return joined_along(jnp.concatenate(gathered, axis=split_at), concat_dim)  7.86 us
    sub x1, other arithmetic, update_state(): new_weight = weight - jnp.float32(0.1) * new_momentum  6.81 us
    split x2, local copies, waits for them, and re-layouts, exchange_in_pieces(): jnp.split(blocks, piece_ends(blocks.shape[split_at], pieces), axis=split_at)  3.63 us
    reduce_sum x1, other arithmetic, body(): total = one_axis_at_a_time(jnp.sum(grad * grad), ROW_COL)  3.59 us
  transfers between devices with their start and end apart: 2, of which 2 were waited for; matrix products, arithmetic and copies ran while one was open for 5% of the time, Pallas kernels for 0%

commit v1 on v0

v1 whole, which is shorter than its diff:
```python
import math

import jax
import jax.numpy as jnp
from jax import lax
from jax.experimental import pallas as pl
from jax.experimental.pallas import tpu as pltpu
from jax.sharding import PartitionSpec as P

D = 8192
FF = 14336
MESH = pl.DeviceIdType.MESH
LIMIT = math.sqrt(D * FF)

NX, NY, NC = 4, 2, 2
PEERS = NX * NY * NC
ROWS, COLS = 64, 896
ZS = 4

STEPS = sorted(
    [(a, b, c) for a in range(NX) for b in range(NY) for c in range(NC) if a or b or c],
    key=lambda s: -min(s[0], NX - s[0]) - s[1],
)
PLANE = [(a, h, b, c) for a in range(NX) for h in range(2) for b in range(NY) for c in range(NC)][1:]


def kernel(g_hbm, m_hbm, w_hbm, nw, nm, g, m, w, out, part, plane, line, load, w_send, w_recv, m_send, m_recv, p_send, p_recv, z_send, z_recv):
    col, row = lax.axis_index("col"), lax.axis_index("row")
    x, y, c = col // (NY * NC), (col // NC) % NY, col % NC
    h, z = row // ZS, row % ZS

    def partner(step):
        a, b, k = step
        return ((x + a) % NX) * (NY * NC) + ((y + b) % NY) * NC + (c + k) % NC

    def columns(p):
        return pl.ds(pl.multiple_of(p * COLS, 128), COLS)

    order = [partner(s) for s in STEPS] + [col]

    loads = {}
    for name, (src, dst) in enumerate(((g_hbm, g), (w_hbm, w), (m_hbm, m))):
        for i, p in enumerate(order):
            loads[name, i] = pltpu.make_async_copy(src.at[:, columns(p)], dst.at[p], load.at[name, i])
    for i in range(PEERS):
        loads[0, i].start()
    for i in range(PEERS):
        loads[1, i].start()
    for i in range(PEERS):
        loads[2, i].start()

    barrier = pltpu.get_barrier_semaphore()
    plane_ids = []
    for a, hh, b, k in PLANE:
        plane_ids.append({"row": ((h + hh) % 2) * ZS + z, "col": partner((a, b, k))})
    line_ids = [{"row": h * ZS + (z + d) % ZS, "col": col} for d in range(1, ZS)]
    for ids in plane_ids + line_ids:
        pl.semaphore_signal(barrier, inc=1, device_id=ids, device_id_type=MESH)

    acc = jnp.zeros((8, COLS), jnp.float32)
    for i, p in enumerate(order):
        loads[0, i].wait()
        for r in range(0, ROWS, 8):
            v = g[p, r : r + 8, :]
            acc = acc + v * v
    acc = jnp.sum(acc, axis=0, keepdims=True)
    own = acc[:, 0:128]
    for j in range(128, COLS, 128):
        own = own + acc[:, j : j + 128]
    part[0] = own
    place = row // ZS * PEERS + col
    plane[place] = own

    pl.semaphore_wait(barrier, len(PLANE) + ZS - 1)

    def plane_copy(j):
        return pltpu.make_async_remote_copy(
            src_ref=part.at[0], dst_ref=plane.at[place], send_sem=p_send.at[j], recv_sem=p_recv.at[j],
            device_id=plane_ids[j], device_id_type=MESH,
        )

    def block_copy(src, dst, send, recv, i):
        return pltpu.make_async_remote_copy(
            src_ref=src.at[order[i]], dst_ref=dst.at[pl.ds(pl.multiple_of(col * ROWS, ROWS), ROWS)],
            send_sem=send.at[i], recv_sem=recv.at[i],
            device_id={"col": order[i]}, device_id_type=MESH,
        )

    small = [plane_copy(j) for j in range(len(PLANE))]
    for copy in small:
        copy.start()
    w_copies = [block_copy(w, nw, w_send, w_recv, i) for i in range(PEERS - 1)]
    for i, copy in enumerate(w_copies):
        loads[1, i].wait()
        copy.start()
    loads[1, PEERS - 1].wait()

    for copy in small:
        copy.wait_recv()
    total = plane[0]
    for j in range(1, 2 * PEERS):
        total = total + plane[j]
    part[1] = total
    line[z] = total
    for i in range(PEERS):
        loads[2, i].wait()
    lines = [
        pltpu.make_async_remote_copy(
            src_ref=part.at[1], dst_ref=line.at[z], send_sem=z_send.at[d], recv_sem=z_recv.at[d],
            device_id=line_ids[d], device_id_type=MESH,
        )
        for d in range(ZS - 1)
    ]
    for copy in lines:
        copy.start()
    for copy in lines:
        copy.wait_recv()
    total = line[0]
    for j in range(1, ZS):
        total = total + line[j]
    total = jnp.sum(total, axis=1, keepdims=True)
    factor = jnp.minimum(jnp.float32(1.0), jnp.float32(LIMIT) / (jnp.sqrt(total) + jnp.float32(1e-06)))

    m_copies = [block_copy(out, nm, m_send, m_recv, i) for i in range(PEERS - 1)]
    for i, p in enumerate(order):
        out[p] = jnp.float32(0.9) * m[p] + factor * g[p]
        if i:
            m_copies[i - 1].start()

    here = pl.ds(pl.multiple_of(col * ROWS, ROWS), ROWS)
    mine = out[col]
    nm[here] = mine
    nw[here] = w[col] - jnp.float32(0.1) * mine
    for i, s in enumerate(STEPS):
        a, b, k = s
        src = partner((NX - a, NY - b, NC - k))
        rows = pl.ds(pl.multiple_of(src * ROWS, ROWS), ROWS)
        w_copies[i].wait_recv()
        m_copies[i].wait_recv()
        nw[rows] = nw[rows] - jnp.float32(0.1) * nm[rows]
    for copy in small + lines + w_copies + m_copies:
        copy.wait_send()


def body(grad, momentum, weight):
    f32 = jnp.float32
    dma = pltpu.SemaphoreType.DMA
    n = PEERS - 1
    blocks = pltpu.VMEM((PEERS, ROWS, COLS), f32)
    return pl.pallas_call(
        kernel,
        out_shape=[jax.ShapeDtypeStruct((PEERS * ROWS, COLS), f32)] * 2,
        in_specs=[pl.BlockSpec(memory_space=pltpu.HBM)] * 3,
        out_specs=[pl.BlockSpec(memory_space=pltpu.VMEM)] * 2,
        scratch_shapes=[
            blocks, blocks, blocks, blocks,
            pltpu.VMEM((2, 1, 128), f32),
            pltpu.VMEM((2 * PEERS, 1, 128), f32),
            pltpu.VMEM((ZS, 1, 128), f32),
            dma((3, PEERS)),
            dma((n,)), dma((n,)), dma((n,)), dma((n,)),
            dma((len(PLANE),)), dma((len(PLANE),)),
            dma((ZS - 1,)), dma((ZS - 1,)),
        ],
        compiler_params=pltpu.CompilerParams(
            collective_id=0, has_side_effects=True, vmem_limit_bytes=40 * 2**20
        ),
    )(grad, momentum, weight)


def solution(mesh):
    return jax.shard_map(
        body,
        mesh=mesh,
        in_specs=(P(("row", "col"), None),) * 3,
        out_specs=(P("row", "col"),) * 2,
        check_vma=False,
    )
```

time: 173 us -> 96.8 us (0.56)
  blocking collectives: 97.3 us -> 0 us
  Pallas kernels: 0 us -> 90.3 us
  waiting for transfers between devices: 40.2 us -> 0 us
  other arithmetic: 18.3 us -> 0 us
  starting transfers between devices: 9.11 us -> 0 us
    pallas_call x0 -> x1, Pallas kernels: none -> 90.3 us  [body(): pl.pallas_call(kernel, out_shape=[jax.ShapeDtypeStruct((PEERS * ROWS, COL...]
    all_to_all x2 -> x0, blocking collectives: 57 us -> none  [exchange_in_pieces(): lax.all_to_all(section, axis, split_axis=0, concat_axis=0, tiled=True)]
    psum x5 -> x0, blocking collectives: 40.3 us -> none  [one_axis_at_a_time(): return functools.reduce(lax.psum, axes, shard)]
    all_to_all x2 -> x0, waiting for transfers between devices: 40.2 us -> none  [exchange_in_pieces(): lax.all_to_all(section, axis, split_axis=0, concat_axis=0, tiled=True)]
    all_to_all x2 -> x0, starting transfers between devices: 9.11 us -> none  [exchange_in_pieces(): lax.all_to_all(section, axis, split_axis=0, concat_axis=0, tiled=True)]
    concatenate x2 -> x0, other arithmetic: 7.86 us -> none  [exchange_in_pieces(): return joined_along(jnp.concatenate(gathered, axis=split_at), concat_dim)]
    sub x1 -> x0, other arithmetic: 6.81 us -> none  [update_state(): new_weight = weight - jnp.float32(0.1) * new_momentum]
    unnamed x0 -> x4, local copies, waits for them, and re-layouts: none -> 5.71 us
  transfers between devices with their start and end apart: 2 -> 0, of which waited for: 2 -> 0; matrix products, arithmetic and copies ran while one was open for 5% -> 0% of each run, Pallas kernels for 0% -> 0%
where the time goes in v1:
time: 96.8 us; the launch traced here: 96.7 us
  Pallas kernels  90.3 us (93%)
  local copies, waits for them, and re-layouts  5.71 us (6%)
    pallas_call x1, Pallas kernels, body(): pl.pallas_call(kernel, out_shape=[jax.ShapeDtypeStruct((PEERS * ROWS, COL...  90.3 us
    unnamed x4, local copies, waits for them, and re-layouts  5.71 us

profile of v1, /device:TPU:1, one launch (start us, length us, event | category | flops | bytes accessed | tf_op | source)
XLA Modules:
  0.0 96.7 jit_solution(1058763438219678254)
XLA Ops:
  0.6 0.0 copy-start
  0.6 2.0 %copy-done = f32[64,14336]{1,0:T(8,128)S(1)} copy-done((f32[64,14336]{1,0:T(8,128)S(1)}, f32[64,14336]{1,0:T(8,128)}, u32[]{:S(2)}) %copy-start) | copy-done | bytes 3670040
  2.7 90.3 %shard_map.50 = (f32[1024,896]{1,0:T(8,128)S(1)}, f32[1024,896]{1,0:T(8,128)S(1)}) custom-call(f32[64,14336]{1,0:T(8,128)S(1)} %copy-done, f32[64,14336]{1,0:T(8,128)} %m_hbm.1, f32[64,14336]{1,0:T(8,128)} %w_hbm.1), custom_call_target="tpu_custom_call" | custom-call | tf_op jit(solution)/shard_map/pallas_call | solution.py:150
  93.0 1.8 %copy.7 = f32[1024,896]{1,0:T(8,128)} copy(f32[1024,896]{1,0:T(8,128)S(1)} %get-tuple-element.4) | data formatting | bytes 7340032
  94.8 1.8 %copy.8 = f32[1024,896]{1,0:T(8,128)} copy(f32[1024,896]{1,0:T(8,128)S(1)} %get-tuple-element.5) | data formatting | bytes 7340032
Async XLA Ops:
  0.6 2.0 %copy-start = (f32[64,14336]{1,0:T(8,128)S(1)}, f32[64,14336]{1,0:T(8,128)}, u32[]{:S(2)}) copy-start(f32[64,14336]{1,0:T(8,128)} %g_hbm.1) | copy-start | bytes 11010052

commit v2 on v1

v2 whole, which is shorter than its diff:
```python
import math

import jax
import jax.numpy as jnp
from jax import lax
from jax.experimental import pallas as pl
from jax.experimental.pallas import tpu as pltpu
from jax.sharding import PartitionSpec as P

D = 8192
FF = 14336
MESH = pl.DeviceIdType.MESH
LIMIT = math.sqrt(D * FF)

NX, NY, NC = 4, 2, 2
NZ = 4
PEERS = NX * NY * NC
ROWS, COLS = 64, 896
PIECES = 8

STEPS = sorted(
    [(a, b, c) for a in range(NX) for b in range(NY) for c in range(NC) if a or b or c],
    key=lambda s: -min(s[0], NX - s[0]) - s[1],
)
FIRST = [(1, 0, 0), (3, 0, 0), (0, 1, 0)]
SPLIT = 32
NEAR = [(1, 0), (3, 0), (0, 1)]
MAIN = 1


def kernel(
    g_hbm, m_hbm, w_hbm, nw, nm, g, m, w, out, part, group, pair, final,
    load, f_send, f_recv, w_send, w_recv, m_send, m_recv, g_send, g_recv, p_send, p_recv, t_send, t_recv, ready,
):
    col, row = lax.axis_index("col"), lax.axis_index("row")
    x, y, c = col // (NY * NC), (col // NC) % NY, col % NC
    h, z = row // NZ, row % NZ

    def place(a, b, k):
        return ((x + a) % NX) * (NY * NC) + ((y + b) % NY) * NC + k

    def partner(step):
        a, b, k = step
        return place(a, b, (c + k) % NC)

    def columns(p):
        return pl.ds(pl.multiple_of(p * COLS, 128), COLS)

    def rows_of(p, start=0, size=ROWS):
        return pl.ds(pl.multiple_of(p * ROWS + start, 8), size)

    near = [{"col": place(a, b, MAIN)} for a, b in NEAR]
    other = {"col": place(0, 0, 1 - c)}
    outside = [
        {"row": (1 - h) * NZ + z, "col": partner((0, 1, 0))},
        {"row": h * NZ + z + 1 - 2 * (z % 2), "col": col},
        {"row": h * NZ + NZ - 1 - z, "col": col},
    ]

    barrier = pltpu.get_barrier_semaphore()
    for ids in near:
        pl.semaphore_signal(barrier, inc=1, device_id=ids, device_id_type=MESH)

    @pl.when(c != MAIN)
    def _():
        pl.semaphore_signal(barrier, inc=1, device_id=other, device_id_type=MESH)
        for ids in outside:
            pl.semaphore_signal(barrier, inc=1, device_id=ids, device_id_type=MESH)

    order = [partner(s) for s in STEPS] + [col]

    def loading(k, i):
        src, dst = ((g_hbm, g), (w_hbm, w), (m_hbm, m))[k]
        return pltpu.make_async_copy(src.at[:, columns(order[i])], dst.at[order[i]], load.at[k, i])

    begin = [STEPS.index(s) for s in FIRST]
    for i in begin:
        loading(1, i).start()
    for i in range(PEERS):
        loading(0, i).start()
    for i in range(PEERS):
        if i not in begin:
            loading(1, i).start()
    for i in range(PEERS):
        loading(2, i).start()

    def block_copy(src, dst, send, recv, i, start, size):
        return pltpu.make_async_remote_copy(
            src_ref=src.at[order[i], pl.ds(start, size)], dst_ref=dst.at[rows_of(col, start, size)],
            send_sem=send, recv_sem=recv, device_id={"col": order[i]}, device_id_type=MESH,
        )

    f_copies = [block_copy(w, nw, f_send.at[j], f_recv.at[j], i, 0, SPLIT) for j, i in enumerate(begin)]
    w_copies = []
    for i in range(PEERS - 1):
        start = SPLIT if i in begin else 0
        w_copies.append(block_copy(w, nw, w_send.at[i], w_recv.at[i], i, start, ROWS - start))
    m_copies = [block_copy(out, nm, m_send.at[i], m_recv.at[i], i, 0, ROWS) for i in range(PEERS - 1)]

    for i in begin:
        loading(1, i).wait()
    @pl.when(c == MAIN)
    def _():
        pl.semaphore_wait(barrier, 2 * len(NEAR) + 1)
        for ids in near:
            pl.semaphore_signal(ready.at[1], inc=1, device_id=ids, device_id_type=MESH)
        pl.semaphore_signal(ready.at[0], inc=1, device_id=other, device_id_type=MESH)

    @pl.when(c != MAIN)
    def _():
        pl.semaphore_wait(ready.at[0], 1)

    for copy in f_copies:
        copy.start()

    @pl.when(c == MAIN)
    def _():
        pl.semaphore_wait(ready.at[1], len(NEAR))
        for ids in near:
            pl.semaphore_signal(ready.at[2], inc=1, device_id=ids, device_id_type=MESH)

    acc = jnp.zeros((8, COLS), jnp.float32)
    for i, p in enumerate(order):
        loading(0, i).wait()
        for r in range(0, ROWS, 8):
            v = g[p, r : r + 8, :]
            acc = acc + v * v
    acc = jnp.sum(acc, axis=0, keepdims=True)
    own = acc[:, 0:128]
    for j in range(128, COLS, 128):
        own = own + acc[:, j : j + 128]
    part[0] = own
    group[col] = own

    @pl.when(c == MAIN)
    def _():
        pl.semaphore_wait(ready.at[2], len(NEAR))
        pl.semaphore_signal(ready.at[1], inc=1, device_id=other, device_id_type=MESH)

    @pl.when(c != MAIN)
    def _():
        pl.semaphore_wait(ready.at[1], 1)

    sums = [
        pltpu.make_async_remote_copy(
            src_ref=part.at[0], dst_ref=group.at[col], send_sem=g_send.at[i], recv_sem=g_recv.at[i],
            device_id={"col": order[i]}, device_id_type=MESH,
        )
        for i in range(PEERS - 1)
    ]
    for copy in sums:
        copy.start()
    for copy in sums:
        copy.wait_send()
    for i in range(PEERS - 1):
        if i not in begin:
            loading(1, i).wait()
        w_copies[i].start()
    loading(1, PEERS - 1).wait()

    for copy in sums:
        copy.wait_recv()
    total = group[0]
    for j in range(1, PEERS):
        total = total + group[j]
    for i in range(PEERS):
        loading(2, i).wait()

    told = pltpu.make_async_remote_copy(
        src_ref=part.at[4], dst_ref=final.at[0], send_sem=t_send.at[0], recv_sem=t_recv.at[0],
        device_id=other, device_id_type=MESH,
    )

    @pl.when(c != MAIN)
    def _():
        pl.semaphore_wait(barrier, len(outside))
        value = total
        copies = []
        for j, ids in enumerate(outside):
            part[1 + j] = value
            copy = pltpu.make_async_remote_copy(
                src_ref=part.at[1 + j], dst_ref=pair.at[j], send_sem=p_send.at[j], recv_sem=p_recv.at[j],
                device_id=ids, device_id_type=MESH,
            )
            copy.start()
            copies.append(copy)
            copy.wait_recv()
            value = value + pair[j]
        part[4] = value
        final[0] = value
        for copy in copies:
            copy.wait_send()
        told.start()
        told.wait_send()

    @pl.when(c == MAIN)
    def _():
        told.wait_recv()

    total = jnp.sum(final[0], axis=1, keepdims=True)
    factor = jnp.minimum(jnp.float32(1.0), jnp.float32(LIMIT) / (jnp.sqrt(total) + jnp.float32(1e-06)))

    for i, p in enumerate(order):
        out[p] = jnp.float32(0.9) * m[p] + factor * g[p]
        if i:
            m_copies[i - 1].start()

    mine = out[col]
    nm[rows_of(col)] = mine
    nw[rows_of(col)] = w[col] - jnp.float32(0.1) * mine
    for i, (a, b, k) in enumerate(STEPS):
        rows = rows_of(partner((NX - a, NY - b, NC - k)))
        if i in begin:
            f_copies[begin.index(i)].wait_recv()
        w_copies[i].wait_recv()
        m_copies[i].wait_recv()
        nw[rows] = nw[rows] - jnp.float32(0.1) * nm[rows]
    for copy in f_copies + w_copies + m_copies:
        copy.wait_send()


def store(nw, nm, nw_hbm, nm_hbm, sem):
    size = nw.shape[0] // PIECES
    copies = []
    for k, (src, dst) in enumerate(((nw, nw_hbm), (nm, nm_hbm))):
        for i in range(PIECES):
            rows = pl.ds(i * size, size)
            copies.append(pltpu.make_async_copy(src.at[rows], dst.at[rows], sem.at[k, i]))
    for copy in copies:
        copy.start()
    for copy in copies:
        copy.wait()


def body(grad, momentum, weight):
    f32 = jnp.float32
    dma = pltpu.SemaphoreType.DMA
    n = PEERS - 1
    blocks = pltpu.VMEM((PEERS, ROWS, COLS), f32)
    outs = [jax.ShapeDtypeStruct((PEERS * ROWS, COLS), f32)] * 2
    landed = pl.pallas_call(
        kernel,
        out_shape=outs,
        in_specs=[pl.BlockSpec(memory_space=pl.ANY)] * 3,
        out_specs=[pl.BlockSpec(memory_space=pltpu.VMEM)] * 2,
        scratch_shapes=[
            blocks, blocks, blocks, blocks,
            pltpu.VMEM((5, 1, 128), f32),
            pltpu.VMEM((PEERS, 1, 128), f32),
            pltpu.VMEM((3, 1, 128), f32),
            pltpu.VMEM((1, 1, 128), f32),
            dma((3, PEERS)),
            dma((len(FIRST),)), dma((len(FIRST),)),
            dma((n,)), dma((n,)), dma((n,)), dma((n,)), dma((n,)), dma((n,)),
            dma((3,)), dma((3,)), dma((1,)), dma((1,)),
            pltpu.SemaphoreType.REGULAR((3,)),
        ],
        compiler_params=pltpu.CompilerParams(
            collective_id=0, has_side_effects=True, vmem_limit_bytes=45 * 2**20
        ),
    )(grad, momentum, weight)
    return pl.pallas_call(
        store,
        out_shape=outs,
        in_specs=[pl.BlockSpec(memory_space=pltpu.VMEM)] * 2,
        out_specs=[pl.BlockSpec(memory_space=pl.ANY)] * 2,
        scratch_shapes=[dma((2, PIECES))],
        compiler_params=pltpu.CompilerParams(vmem_limit_bytes=2 * 2**20),
    )(*landed)


def solution(mesh):
    return jax.shard_map(
        body,
        mesh=mesh,
        in_specs=(P(("row", "col"), None),) * 3,
        out_specs=(P("row", "col"),) * 2,
        check_vma=False,
    )
```

time: 96.8 us -> 91.5 us (0.945)
  local copies, waits for them, and re-layouts: 5.71 us -> 0 us
    unnamed x4 -> x0, local copies, waits for them, and re-layouts: 5.71 us -> none
    pallas_call x1 -> x2, Pallas kernels: 90.3 us -> 90.8 us  [the longest x1 87.7 us: body(): pl.pallas_call(kernel, out_shape=outs, in_specs=[pl.BlockSpec(memory_spac...]
where the time goes in v2:
time: 91.5 us; the launch traced here: 91.4 us
  Pallas kernels  90.8 us (99%)
    pallas_call x1, Pallas kernels, body(): pl.pallas_call(kernel, out_shape=outs, in_specs=[pl.BlockSpec(memory_spac...  87.7 us
    pallas_call x1, Pallas kernels, body(): pl.pallas_call(store, out_shape=outs, in_specs=[pl.BlockSpec(memory_space...  3.11 us

profile of v2, /device:TPU:1, one launch (start us, length us, event | category | flops | bytes accessed | tf_op | source)
XLA Modules:
  0.0 91.4 jit_solution(7584930968548814897)
XLA Ops:
  0.6 87.7 %shard_map.50 = (f32[1024,896]{1,0:T(8,128)S(1)}, f32[1024,896]{1,0:T(8,128)S(1)}) custom-call(f32[64,14336]{1,0:T(8,128)} %g_hbm.1, f32[64,14336]{1,0:T(8,128)} %m_hbm.1, f32[64,14336]{1,0:T(8,128)} %w_hbm.1), custom_call_target="tpu_custom_call" | custom-call | tf_op jit(solution)/shard_map/pallas_call | solution.py:241
  88.3 3.1 %shard_map.51 = (f32[1024,896]{1,0:T(8,128)}, f32[1024,896]{1,0:T(8,128)}) custom-call(f32[1024,896]{1,0:T(8,128)S(1)} %get-tuple-element.4.nw, f32[1024,896]{1,0:T(8,128)S(1)} %get-tuple-element.5.nm), custom_call_target="tpu_custom_call" | custom-call | tf_op jit(solution)/shard_map/pallas_call | solution.py:262

commit v3 on v2

v3 whole, which is shorter than its diff:
```python
import math

import jax
import jax.numpy as jnp
from jax import lax
from jax.experimental import pallas as pl
from jax.experimental.pallas import tpu as pltpu
from jax.sharding import PartitionSpec as P

D = 8192
FF = 14336
MESH = pl.DeviceIdType.MESH
LIMIT = math.sqrt(D * FF)

NX, NY, NC = 4, 2, 2
NZ = 4
PEERS = NX * NY * NC
ROWS, COLS = 64, 896
PIECES = 8

STEPS = sorted(
    [(a, b, c) for a in range(NX) for b in range(NY) for c in range(NC) if a or b or c],
    key=lambda s: -min(s[0], NX - s[0]) - s[1],
)
FIRST = [(1, 0, 0), (3, 0, 0), (0, 1, 0)]
SPLIT = 32
NEAR = [(1, 0), (3, 0), (0, 1)]
MAIN = 1
LOADS = 4


def kernel(
    g_hbm, m_hbm, w_hbm, nw, nm, g, m, w, out, part, group, pair, final,
    load, send, recv, p_send, p_recv, t_send, t_recv, ready,
):
    col, row = lax.axis_index("col"), lax.axis_index("row")
    x, y, c = col // (NY * NC), (col // NC) % NY, col % NC
    h, z = row // NZ, row % NZ

    def place(a, b, k):
        return ((x + a) % NX) * (NY * NC) + ((y + b) % NY) * NC + k

    def partner(step):
        a, b, k = step
        return place(a, b, (c + k) % NC)

    def columns(p):
        return pl.ds(pl.multiple_of(p * COLS, 128), COLS)

    def rows_of(p, start=0, size=ROWS):
        return pl.ds(pl.multiple_of(p * ROWS + start, 8), size)

    def wait_for(ref, sem):
        pltpu.make_async_copy(ref, ref, sem).wait()

    near = [{"col": place(a, b, MAIN)} for a, b in NEAR]
    other = {"col": place(0, 0, 1 - c)}
    outside = [
        {"row": (1 - h) * NZ + z, "col": partner((0, 1, 0))},
        {"row": h * NZ + z + 1 - 2 * (z % 2), "col": col},
        {"row": h * NZ + NZ - 1 - z, "col": col},
    ]

    barrier = pltpu.get_barrier_semaphore()
    for ids in near:
        pl.semaphore_signal(barrier, inc=1, device_id=ids, device_id_type=MESH)

    @pl.when(c != MAIN)
    def _():
        pl.semaphore_signal(barrier, inc=1, device_id=other, device_id_type=MESH)
        for ids in outside:
            pl.semaphore_signal(barrier, inc=1, device_id=ids, device_id_type=MESH)

    order = [partner(s) for s in STEPS] + [col]
    begin = [STEPS.index(s) for s in FIRST]
    later = [i for i in range(PEERS) if i not in begin]

    def load_rows(src, dst, k):
        size = ROWS // LOADS
        for j in range(LOADS):
            rows = pl.ds(j * size, size)
            pltpu.make_async_copy(src.at[rows], dst.at[rows], load.at[k]).start()

    for i in begin:
        pltpu.make_async_copy(w_hbm.at[:, columns(order[i])], w.at[order[i]], load.at[0]).start()
    load_rows(g_hbm, g, 1)
    for i in later:
        pltpu.make_async_copy(w_hbm.at[:, columns(order[i])], w.at[order[i]], load.at[2]).start()
    load_rows(m_hbm, m, 3)

    def block_copy(src, dst, k, i, start=0, size=ROWS):
        return pltpu.make_async_remote_copy(
            src_ref=src.at[order[i], pl.ds(start, size)], dst_ref=dst.at[rows_of(col, start, size)],
            send_sem=send.at[k], recv_sem=recv.at[k], device_id={"col": order[i]}, device_id_type=MESH,
        )

    wait_for(w.at[pl.ds(0, len(begin))], load.at[0])

    @pl.when(c == MAIN)
    def _():
        pl.semaphore_wait(barrier, 2 * len(NEAR) + 1)
        for ids in near:
            pl.semaphore_signal(ready.at[1], inc=1, device_id=ids, device_id_type=MESH)
        pl.semaphore_signal(ready.at[0], inc=1, device_id=other, device_id_type=MESH)

    @pl.when(c != MAIN)
    def _():
        pl.semaphore_wait(ready.at[0], 1)

    for i in begin:
        block_copy(w, nw, 0, i, 0, SPLIT).start()

    @pl.when(c == MAIN)
    def _():
        pl.semaphore_wait(ready.at[1], len(NEAR))
        for ids in near:
            pl.semaphore_signal(ready.at[2], inc=1, device_id=ids, device_id_type=MESH)

    wait_for(g, load.at[1])
    acc = jnp.zeros((8, COLS), jnp.float32)
    for i in range(PEERS):
        for r in range(0, ROWS, 8):
            v = g[r : r + 8, i * COLS : (i + 1) * COLS]
            acc = acc + v * v
    acc = jnp.sum(acc, axis=0, keepdims=True)
    own = acc[:, 0:128]
    for j in range(128, COLS, 128):
        own = own + acc[:, j : j + 128]
    part[0] = own
    group[col] = own

    @pl.when(c == MAIN)
    def _():
        pl.semaphore_wait(ready.at[2], len(NEAR))
        pl.semaphore_signal(ready.at[1], inc=1, device_id=other, device_id_type=MESH)

    @pl.when(c != MAIN)
    def _():
        pl.semaphore_wait(ready.at[1], 1)

    for i in range(PEERS - 1):
        pltpu.make_async_remote_copy(
            src_ref=part.at[0], dst_ref=group.at[col], send_sem=send.at[2], recv_sem=recv.at[2],
            device_id={"col": order[i]}, device_id_type=MESH,
        ).start()
    wait_for(group.at[pl.ds(0, PEERS - 1)], send.at[2])
    wait_for(w.at[pl.ds(0, len(later))], load.at[2])

    def send_weight():
        for i in range(PEERS - 1):
            start = SPLIT if i in begin else 0
            if start < ROWS:
                block_copy(w, nw, 0, i, start, ROWS - start).start()

    send_weight()
    wait_for(group.at[pl.ds(0, PEERS - 1)], recv.at[2])
    total = group[0]
    for j in range(1, PEERS):
        total = total + group[j]

    told = pltpu.make_async_remote_copy(
        src_ref=part.at[4], dst_ref=final.at[0], send_sem=t_send, recv_sem=t_recv,
        device_id=other, device_id_type=MESH,
    )

    @pl.when(c != MAIN)
    def _():
        pl.semaphore_wait(barrier, len(outside))
        value = total
        for j, ids in enumerate(outside):
            part[1 + j] = value
            copy = pltpu.make_async_remote_copy(
                src_ref=part.at[1 + j], dst_ref=pair.at[j], send_sem=p_send.at[j], recv_sem=p_recv.at[j],
                device_id=ids, device_id_type=MESH,
            )
            copy.start()
            copy.wait()
            value = value + pair[j]
        part[4] = value
        final[0] = value
        told.start()
        told.wait_send()

    @pl.when(c == MAIN)
    def _():
        told.wait_recv()

    total = jnp.sum(final[0], axis=1, keepdims=True)
    factor = jnp.minimum(jnp.float32(1.0), jnp.float32(LIMIT) / (jnp.sqrt(total) + jnp.float32(1e-06)))

    wait_for(m, load.at[3])
    for i, p in enumerate(order):
        out[p] = jnp.float32(0.9) * m[:, columns(p)] + factor * g[:, columns(p)]
        if i:
            block_copy(out, nm, 1, i - 1).start()

    nm[rows_of(col)] = out[col]
    nw[rows_of(col)] = w[col]
    for k, ref in enumerate((nw, nm)):
        wait_for(ref.at[pl.ds(0, (PEERS - 1) * ROWS)], recv.at[k])
    for k, ref in enumerate((nw, nm)):
        wait_for(ref.at[pl.ds(0, (PEERS - 1) * ROWS)], send.at[k])


def store(w, nm, nw_hbm, nm_hbm, nw, sem):
    size = w.shape[0] // PIECES

    def piece(src, dst, k, i):
        rows = pl.ds(i * size, size)
        return pltpu.make_async_copy(src.at[rows], dst.at[rows], sem.at[k])

    for i in range(PIECES):
        piece(nm, nm_hbm, 0, i).start()
    for i in range(PIECES):
        rows = pl.ds(i * size, size)
        nw[rows] = w[rows] - jnp.float32(0.1) * nm[rows]
        if i:
            piece(nw, nw_hbm, 1, i - 1).start()
    piece(nw, nw_hbm, 1, PIECES - 1).start()
    pltpu.make_async_copy(nm, nm_hbm, sem.at[0]).wait()
    pltpu.make_async_copy(nw, nw_hbm, sem.at[1]).wait()


def body(grad, momentum, weight):
    f32 = jnp.float32
    dma = pltpu.SemaphoreType.DMA
    blocks = pltpu.VMEM((PEERS, ROWS, COLS), f32)
    whole = pltpu.VMEM((ROWS, PEERS * COLS), f32)
    outs = [jax.ShapeDtypeStruct((PEERS * ROWS, COLS), f32)] * 2
    landed = pl.pallas_call(
        kernel,
        out_shape=outs,
        in_specs=[pl.BlockSpec(memory_space=pl.ANY)] * 3,
        out_specs=[pl.BlockSpec(memory_space=pltpu.VMEM)] * 2,
        scratch_shapes=[
            whole, whole, blocks, blocks,
            pltpu.VMEM((5, 1, 128), f32),
            pltpu.VMEM((PEERS, 1, 128), f32),
            pltpu.VMEM((3, 1, 128), f32),
            pltpu.VMEM((1, 1, 128), f32),
            dma((4,)), dma((3,)), dma((3,)), dma((3,)), dma((3,)), dma, dma,
            pltpu.SemaphoreType.REGULAR((3,)),
        ],
        compiler_params=pltpu.CompilerParams(
            collective_id=0, has_side_effects=True, vmem_limit_bytes=45 * 2**20
        ),
    )(grad, momentum, weight)
    return pl.pallas_call(
        store,
        out_shape=outs,
        in_specs=[pl.BlockSpec(memory_space=pltpu.VMEM)] * 2,
        out_specs=[pl.BlockSpec(memory_space=pl.ANY)] * 2,
        scratch_shapes=[pltpu.VMEM((PEERS * ROWS, COLS), f32), dma((2,))],
        compiler_params=pltpu.CompilerParams(vmem_limit_bytes=8 * 2**20),
    )(*landed)


def solution(mesh):
    return jax.shard_map(
        body,
        mesh=mesh,
        in_specs=(P(("row", "col"), None),) * 3,
        out_specs=(P("row", "col"),) * 2,
        check_vma=False,
    )
```

time: 91.5 us -> 89.9 us (0.983)
  Pallas kernels: 90.8 us -> 89.2 us
    pallas_call x1, Pallas kernels: 87.7 us -> 86.2 us  [body(): pl.pallas_call(kernel, out_shape=outs, in_specs=[pl.BlockSpec(memory_spac...]
where the time goes in v3:
time: 89.9 us; the launch traced here: 89.8 us
  Pallas kernels  89.2 us (99%)
    pallas_call x1, Pallas kernels, body(): pl.pallas_call(kernel, out_shape=outs, in_specs=[pl.BlockSpec(memory_spac...  86.2 us
    pallas_call x1, Pallas kernels, body(): pl.pallas_call(store, out_shape=outs, in_specs=[pl.BlockSpec(memory_space...  2.98 us

profile of v3, /device:TPU:1, one launch (start us, length us, event | category | flops | bytes accessed | tf_op | source)
XLA Modules:
  0.0 89.8 jit_solution(9552416698317499037)
XLA Ops:
  0.6 86.2 %shard_map.50 = (f32[1024,896]{1,0:T(8,128)S(1)}, f32[1024,896]{1,0:T(8,128)S(1)}) custom-call(f32[64,14336]{1,0:T(8,128)} %g_hbm.1, f32[64,14336]{1,0:T(8,128)} %m_hbm.1, f32[64,14336]{1,0:T(8,128)} %w_hbm.1), custom_call_target="tpu_custom_call" | custom-call | tf_op jit(solution)/shard_map/pallas_call | solution.py:230
  86.8 3.0 %shard_map.51 = (f32[1024,896]{1,0:T(8,128)}, f32[1024,896]{1,0:T(8,128)}) custom-call(f32[1024,896]{1,0:T(8,128)S(1)} %get-tuple-element.4.w, f32[1024,896]{1,0:T(8,128)S(1)} %get-tuple-element.5.nm), custom_call_target="tpu_custom_call" | custom-call | tf_op jit(solution)/shard_map/pallas_call | solution.py:248

commit v4 on v3

--- a/solution.py
+++ b/solution.py
@@ -18,12 +18,13 @@
 ROWS, COLS = 64, 896
 PIECES = 8
 
-STEPS = sorted(
-    [(a, b, c) for a in range(NX) for b in range(NY) for c in range(NC) if a or b or c],
-    key=lambda s: -min(s[0], NX - s[0]) - s[1],
-)
+STEPS = [
+    (2, 1, 1), (2, 1, 0), (1, 1, 1), (1, 1, 0), (2, 0, 1), (2, 0, 0), (3, 1, 1), (3, 1, 0),
+    (0, 1, 1), (0, 1, 0), (1, 0, 1), (1, 0, 0), (3, 0, 1), (3, 0, 0), (0, 0, 1),
+]
 FIRST = [(1, 0, 0), (3, 0, 0), (0, 1, 0)]
-SPLIT = 32
+SECOND = [(0, 1, 1), (1, 0, 1), (3, 0, 1), (0, 0, 1)]
+THIRD = STEPS[:8]
 NEAR = [(1, 0), (3, 0), (0, 1)]
 MAIN = 1
 LOADS = 4
@@ -47,8 +48,8 @@
     def columns(p):
         return pl.ds(pl.multiple_of(p * COLS, 128), COLS)
 
-    def rows_of(p, start=0, size=ROWS):
-        return pl.ds(pl.multiple_of(p * ROWS + start, 8), size)
+    def rows_of(p):
+        return pl.ds(pl.multiple_of(p * ROWS, ROWS), ROWS)
 
     def wait_for(ref, sem):
         pltpu.make_async_copy(ref, ref, sem).wait()
@@ -72,8 +73,8 @@
             pl.semaphore_signal(barrier, inc=1, device_id=ids, device_id_type=MESH)
 
     order = [partner(s) for s in STEPS] + [col]
-    begin = [STEPS.index(s) for s in FIRST]
-    later = [i for i in range(PEERS) if i not in begin]
+    first, second, third = ([STEPS.index(s) for s in part_of] for part_of in (FIRST, SECOND, THIRD))
+    later = second + third + [PEERS - 1]
 
     def load_rows(src, dst, k):
         size = ROWS // LOADS
@@ -81,20 +82,17 @@
             rows = pl.ds(j * size, size)
             pltpu.make_async_copy(src.at[rows], dst.at[rows], load.at[k]).start()
 
-    for i in begin:
+    for i in first:
         pltpu.make_async_copy(w_hbm.at[:, columns(order[i])], w.at[order[i]], load.at[0]).start()
     load_rows(g_hbm, g, 1)
-    for i in later:
-        pltpu.make_async_copy(w_hbm.at[:, columns(order[i])], w.at[order[i]], load.at[2]).start()
-    load_rows(m_hbm, m, 3)
-
-    def block_copy(src, dst, k, i, start=0, size=ROWS):
+
+    def block_copy(src, dst, k, i):
         return pltpu.make_async_remote_copy(
-            src_ref=src.at[order[i], pl.ds(start, size)], dst_ref=dst.at[rows_of(col, start, size)],
+            src_ref=src.at[order[i]], dst_ref=dst.at[rows_of(col)],
             send_sem=send.at[k], recv_sem=recv.at[k], device_id={"col": order[i]}, device_id_type=MESH,
         )
 
-    wait_for(w.at[pl.ds(0, len(begin))], load.at[0])
+    wait_for(w.at[pl.ds(0, len(first))], load.at[0])
 
     @pl.when(c == MAIN)
     def _():
@@ -107,8 +105,11 @@
     def _():
         pl.semaphore_wait(ready.at[0], 1)
 
-    for i in begin:
-        block_copy(w, nw, 0, i, 0, SPLIT).start()
+    for i in first:
+        block_copy(w, nw, 0, i).start()
+    for i in later:
+        pltpu.make_async_copy(w_hbm.at[:, columns(order[i])], w.at[order[i]], load.at[2]).start()
+    load_rows(m_hbm, m, 3)
 
     @pl.when(c == MAIN)
     def _():
@@ -146,14 +147,13 @@
     wait_for(group.at[pl.ds(0, PEERS - 1)], send.at[2])
     wait_for(w.at[pl.ds(0, len(later))], load.at[2])
 
-    def send_weight():
-        for i in range(PEERS - 1):
-            start = SPLIT if i in begin else 0
-            if start < ROWS:
-                block_copy(w, nw, 0, i, start, ROWS - start).start()
-
-    send_weight()
+    for i in second:
+        block_copy(w, nw, 0, i).start()
+
     wait_for(group.at[pl.ds(0, PEERS - 1)], recv.at[2])
+    for i in third:
+        block_copy(w, nw, 0, i).start()
+
     total = group[0]
     for j in range(1, PEERS):
         total = total + group[j]

time: 89.9 us -> 89.2 us (level)
  no operation moved by 1% of the time
where the time goes in v4:
time: 89.2 us; the launch traced here: 89.1 us
  Pallas kernels  88.5 us (99%)
    pallas_call x1, Pallas kernels, body(): pl.pallas_call(kernel, out_shape=outs, in_specs=[pl.BlockSpec(memory_spac...  85.5 us
    pallas_call x1, Pallas kernels, body(): pl.pallas_call(store, out_shape=outs, in_specs=[pl.BlockSpec(memory_space...  2.98 us

profile of v4, /device:TPU:1, one launch (start us, length us, event | category | flops | bytes accessed | tf_op | source)
XLA Modules:
  0.0 89.1 jit_solution(9976097752317537526)
XLA Ops:
  0.6 85.5 %shard_map.50 = (f32[1024,896]{1,0:T(8,128)S(1)}, f32[1024,896]{1,0:T(8,128)S(1)}) custom-call(f32[64,14336]{1,0:T(8,128)} %g_hbm.1, f32[64,14336]{1,0:T(8,128)} %m_hbm.1, f32[64,14336]{1,0:T(8,128)} %w_hbm.1), custom_call_target="tpu_custom_call" | custom-call | tf_op jit(solution)/shard_map/pallas_call | solution.py:230
  86.1 3.0 %shard_map.51 = (f32[1024,896]{1,0:T(8,128)}, f32[1024,896]{1,0:T(8,128)}) custom-call(f32[1024,896]{1,0:T(8,128)S(1)} %get-tuple-element.4.w, f32[1024,896]{1,0:T(8,128)S(1)} %get-tuple-element.5.nm), custom_call_target="tpu_custom_call" | custom-call | tf_op jit(solution)/shard_map/pallas_call | solution.py:248

commit v5 on v4

--- a/solution.py
+++ b/solution.py
@@ -54,7 +54,7 @@
     def wait_for(ref, sem):
         pltpu.make_async_copy(ref, ref, sem).wait()
 
-    near = [{"col": place(a, b, MAIN)} for a, b in NEAR]
+    near = [{"col": place(a, b, c)} for a, b in NEAR]
     other = {"col": place(0, 0, 1 - c)}
     outside = [
         {"row": (1 - h) * NZ + z, "col": partner((0, 1, 0))},
@@ -62,14 +62,21 @@
         {"row": h * NZ + NZ - 1 - z, "col": col},
     ]
 
+    asks = [h == 0, z % 2 == 0, z < NZ // 2]
+    asked = h + z % 2 + z // (NZ // 2)
+
     barrier = pltpu.get_barrier_semaphore()
     for ids in near:
         pl.semaphore_signal(barrier, inc=1, device_id=ids, device_id_type=MESH)
 
-    @pl.when(c != MAIN)
+    @pl.when(c == MAIN)
     def _():
         pl.semaphore_signal(barrier, inc=1, device_id=other, device_id_type=MESH)
-        for ids in outside:
+
+    for ask, ids in zip(asks, outside):
+
+        @pl.when((c != MAIN) & ask)
+        def _():
             pl.semaphore_signal(barrier, inc=1, device_id=ids, device_id_type=MESH)
 
     order = [partner(s) for s in STEPS] + [col]
@@ -96,14 +103,12 @@
 
     @pl.when(c == MAIN)
     def _():
-        pl.semaphore_wait(barrier, 2 * len(NEAR) + 1)
-        for ids in near:
-            pl.semaphore_signal(ready.at[1], inc=1, device_id=ids, device_id_type=MESH)
+        pl.semaphore_wait(barrier, len(NEAR))
+
+    @pl.when(c != MAIN)
+    def _():
+        pl.semaphore_wait(barrier, len(NEAR) + 1 + asked)
         pl.semaphore_signal(ready.at[0], inc=1, device_id=other, device_id_type=MESH)
-
-    @pl.when(c != MAIN)
-    def _():
-        pl.semaphore_wait(ready.at[0], 1)
 
     for i in first:
         block_copy(w, nw, 0, i).start()
@@ -113,9 +118,18 @@
 
     @pl.when(c == MAIN)
     def _():
+        pl.semaphore_wait(ready.at[0], 1)
+        for ids in near:
+            pl.semaphore_signal(ready.at[1], inc=1, device_id=ids, device_id_type=MESH)
         pl.semaphore_wait(ready.at[1], len(NEAR))
         for ids in near:
             pl.semaphore_signal(ready.at[2], inc=1, device_id=ids, device_id_type=MESH)
+
+    for j, (ask, ids) in enumerate(zip(asks, outside)):
+
+        @pl.when((c != MAIN) & jnp.logical_not(ask))
+        def _():
+            pl.semaphore_signal(ready.at[3 + j], inc=1, device_id=ids, device_id_type=MESH)
 
     wait_for(g, load.at[1])
     acc = jnp.zeros((8, COLS), jnp.float32)
@@ -165,10 +179,14 @@
 
     @pl.when(c != MAIN)
     def _():
-        pl.semaphore_wait(barrier, len(outside))
         value = total
         for j, ids in enumerate(outside):
             part[1 + j] = value
+
+            @pl.when(asks[j])
+            def _():
+                pl.semaphore_wait(ready.at[3 + j], 1)
+
             copy = pltpu.make_async_remote_copy(
                 src_ref=part.at[1 + j], dst_ref=pair.at[j], send_sem=p_send.at[j], recv_sem=p_recv.at[j],
                 device_id=ids, device_id_type=MESH,
@@ -239,7 +257,7 @@
             pltpu.VMEM((3, 1, 128), f32),
             pltpu.VMEM((1, 1, 128), f32),
             dma((4,)), dma((3,)), dma((3,)), dma((3,)), dma((3,)), dma, dma,
-            pltpu.SemaphoreType.REGULAR((3,)),
+            pltpu.SemaphoreType.REGULAR((6,)),
         ],
         compiler_params=pltpu.CompilerParams(
             collective_id=0, has_side_effects=True, vmem_limit_bytes=45 * 2**20

time: 89.2 us -> 89.2 us (level)
  no operation moved by 1% of the time
where the time goes in v5:
time: 89.2 us; the launch traced here: 89.1 us
  Pallas kernels  88.5 us (99%)
    pallas_call x1, Pallas kernels, body(): pl.pallas_call(kernel, out_shape=outs, in_specs=[pl.BlockSpec(memory_spac...  85.5 us
    pallas_call x1, Pallas kernels, body(): pl.pallas_call(store, out_shape=outs, in_specs=[pl.BlockSpec(memory_space...  2.98 us

profile of v5, /device:TPU:1, one launch (start us, length us, event | category | flops | bytes accessed | tf_op | source)
XLA Modules:
  0.0 89.1 jit_solution(6385241813962513935)
XLA Ops:
  0.6 85.5 %shard_map.50 = (f32[1024,896]{1,0:T(8,128)S(1)}, f32[1024,896]{1,0:T(8,128)S(1)}) custom-call(f32[64,14336]{1,0:T(8,128)} %g_hbm.1, f32[64,14336]{1,0:T(8,128)} %m_hbm.1, f32[64,14336]{1,0:T(8,128)} %w_hbm.1), custom_call_target="tpu_custom_call" | custom-call | tf_op jit(solution)/shard_map/pallas_call | solution.py:248
  86.1 3.0 %shard_map.51 = (f32[1024,896]{1,0:T(8,128)}, f32[1024,896]{1,0:T(8,128)}) custom-call(f32[1024,896]{1,0:T(8,128)S(1)} %get-tuple-element.4.w, f32[1024,896]{1,0:T(8,128)S(1)} %get-tuple-element.5.nm), custom_call_target="tpu_custom_call" | custom-call | tf_op jit(solution)/shard_map/pallas_call | solution.py:266

commit v6 on v5

--- a/solution.py
+++ b/solution.py
@@ -54,6 +54,13 @@
     def wait_for(ref, sem):
         pltpu.make_async_copy(ref, ref, sem).wait()
 
+    order = [partner(s) for s in STEPS] + [col]
+    first, second, third = ([STEPS.index(s) for s in part_of] for part_of in (FIRST, SECOND, THIRD))
+    later = second + third + [PEERS - 1]
+
+    for i in first:
+        pltpu.make_async_copy(w_hbm.at[:, columns(order[i])], w.at[order[i]], load.at[0]).start()
+
     near = [{"col": place(a, b, c)} for a, b in NEAR]
     other = {"col": place(0, 0, 1 - c)}
     outside = [
@@ -79,18 +86,12 @@
         def _():
             pl.semaphore_signal(barrier, inc=1, device_id=ids, device_id_type=MESH)
 
-    order = [partner(s) for s in STEPS] + [col]
-    first, second, third = ([STEPS.index(s) for s in part_of] for part_of in (FIRST, SECOND, THIRD))
-    later = second + third + [PEERS - 1]
-
     def load_rows(src, dst, k):
         size = ROWS // LOADS
         for j in range(LOADS):
             rows = pl.ds(j * size, size)
             pltpu.make_async_copy(src.at[rows], dst.at[rows], load.at[k]).start()
 
-    for i in first:
-        pltpu.make_async_copy(w_hbm.at[:, columns(order[i])], w.at[order[i]], load.at[0]).start()
     load_rows(g_hbm, g, 1)
 
     def block_copy(src, dst, k, i):

time: 89.2 us -> 89.2 us (level)
  no operation moved by 1% of the time
where the time goes in v6:
time: 89.2 us; the launch traced here: 89.1 us
  Pallas kernels  88.5 us (99%)
    pallas_call x1, Pallas kernels, body(): pl.pallas_call(kernel, out_shape=outs, in_specs=[pl.BlockSpec(memory_spac...  85.5 us
    pallas_call x1, Pallas kernels, body(): pl.pallas_call(store, out_shape=outs, in_specs=[pl.BlockSpec(memory_space...  2.98 us

profile of v6, /device:TPU:1, one launch (start us, length us, event | category | flops | bytes accessed | tf_op | source)
XLA Modules:
  0.0 89.1 jit_solution(2471212404096268)
XLA Ops:
  0.6 85.5 %shard_map.50 = (f32[1024,896]{1,0:T(8,128)S(1)}, f32[1024,896]{1,0:T(8,128)S(1)}) custom-call(f32[64,14336]{1,0:T(8,128)} %g_hbm.1, f32[64,14336]{1,0:T(8,128)} %m_hbm.1, f32[64,14336]{1,0:T(8,128)} %w_hbm.1), custom_call_target="tpu_custom_call" | custom-call | tf_op jit(solution)/shard_map/pallas_call | solution.py:249
  86.1 3.0 %shard_map.51 = (f32[1024,896]{1,0:T(8,128)}, f32[1024,896]{1,0:T(8,128)}) custom-call(f32[1024,896]{1,0:T(8,128)S(1)} %get-tuple-element.4.w, f32[1024,896]{1,0:T(8,128)S(1)} %get-tuple-element.5.nm), custom_call_target="tpu_custom_call" | custom-call | tf_op jit(solution)/shard_map/pallas_call | solution.py:267

commit v7 on v6

--- a/solution.py
+++ b/solution.py
@@ -16,7 +16,7 @@
 NZ = 4
 PEERS = NX * NY * NC
 ROWS, COLS = 64, 896
-PIECES = 8
+PIECES = 16
 
 STEPS = [
     (2, 1, 1), (2, 1, 0), (1, 1, 1), (1, 1, 0), (2, 0, 1), (2, 0, 0), (3, 1, 1), (3, 1, 0),

time: 89.2 us -> 89.2 us (level)
  no operation moved by 1% of the time
where the time goes in v7:
time: 89.2 us; the launch traced here: 89.1 us
  Pallas kernels  88.5 us (99%)
    pallas_call x1, Pallas kernels, body(): pl.pallas_call(kernel, out_shape=outs, in_specs=[pl.BlockSpec(memory_spac...  85.5 us
    pallas_call x1, Pallas kernels, body(): pl.pallas_call(store, out_shape=outs, in_specs=[pl.BlockSpec(memory_space...  2.97 us

profile of v7, /device:TPU:1, one launch (start us, length us, event | category | flops | bytes accessed | tf_op | source)
XLA Modules:
  0.0 89.1 jit_solution(3798069034190622338)
XLA Ops:
  0.6 85.5 %shard_map.50 = (f32[1024,896]{1,0:T(8,128)S(1)}, f32[1024,896]{1,0:T(8,128)S(1)}) custom-call(f32[64,14336]{1,0:T(8,128)} %g_hbm.1, f32[64,14336]{1,0:T(8,128)} %m_hbm.1, f32[64,14336]{1,0:T(8,128)} %w_hbm.1), custom_call_target="tpu_custom_call" | custom-call | tf_op jit(solution)/shard_map/pallas_call | solution.py:249
  86.1 3.0 %shard_map.51 = (f32[1024,896]{1,0:T(8,128)}, f32[1024,896]{1,0:T(8,128)}) custom-call(f32[1024,896]{1,0:T(8,128)S(1)} %get-tuple-element.4.w, f32[1024,896]{1,0:T(8,128)S(1)} %get-tuple-element.5.nm), custom_call_target="tpu_custom_call" | custom-call | tf_op jit(solution)/shard_map/pallas_call | solution.py:267
